TPU v7x, 128 devices: a whole 4x4x4 slice. The times are simulated.
128 devices in a mesh: dp: 16 (over z, x_lo, core), mp: 8 (over x_hi, y).
Axes of the slice: x: 4 (x_hi: 2, x_lo: 2; x = x_hi * 2 + x_lo), y: 4, z: 4, core: 2. Of those that a mesh axis runs over, the one named last changes fastest.
Arguments:
- master: float32 [8192, 5120], P('dp', 'mp'), may hold values from -60 to 60
- moment_first: float32 [8192, 5120], P('dp', 'mp'), may hold values from -0.06 to 0.06
- moment_second: float32 [8192, 5120], P('dp', 'mp'), may hold values from 1e-05 to 0.001
- gradients: float32 [8192, 5120], P('dp', 'mp'), may hold values from -0.2 to 0.2
- step_count: int32 [1], replicated, may hold values from 1 to 10
- tensor_rows: int32 [24], replicated, may hold values from 1 to 1280, 8192 in all
- decay_mask: int32 [24], replicated, may hold values 0 or 1
Outputs:
- new_master: float32 [8192, 5120], P('dp', 'mp')
- new_first: float32 [8192, 5120], P('dp', 'mp')
- new_second: float32 [8192, 5120], P('dp', 'mp')
- compute_weights: bfloat16 [8192, 5120], P(None, 'mp')
Inputs may be any that keep to these rules, and one draw needn't show every extreme that they name: `tensor_rows`: the rows sum to 8192; the largest tensor has 1280 rows.
All inputs are finite; a program needn't handle non-finite values.
Results may differ from a plain program's by a relative error of at most 0.0004.
Values may be sent and summed in bfloat16 or wider, within the bound.
A program may use at most 128 MiB of HBM per device.

v0:
```python
import jax
import jax.numpy as jnp
from jax import lax
from jax.sharding import PartitionSpec as P

beta_first = 0.9
beta_second = 0.999
adam_epsilon = 1e-06
decay_rate = 0.3
learn_rate = 0.3
norm_epsilon = 1e-06


def copy_for_each(x, axis):
    size = lax.axis_size(axis)
    return lax.all_to_all(jnp.broadcast_to(x[None], (size, *x.shape)), axis, 0, 0, tiled=True)


def over_copies(x, axis):
    everything = copy_for_each(x, axis)
    return jnp.sum(everything, axis=0)


def together(arrays, axis):
    flat, at, gathered = (jnp.concatenate([a.reshape(-1) for a in arrays]), 0, [])
    subtotal = over_copies(flat, axis)
    for a in arrays:
        gathered.append(subtotal[at : at + a.size].reshape(a.shape))
        at += a.size
    return tuple(gathered)


def membership(first_row, count, offsets, tensor_rows):
    row_ids = first_row + jnp.arange(count, dtype=jnp.int32)
    inside = (row_ids[None, :] >= offsets[:, None]) & (
        row_ids[None, :] < (offsets + tensor_rows)[:, None]
    )
    return inside.astype(jnp.float32)


def local(master, moment_first, moment_second, gradients, step_count, tensor_rows, decay_mask):
    rows_dev = master.shape[0]
    steps = step_count[0].astype(jnp.float32)
    new_first = beta_first * moment_first + (1.0 - beta_first) * gradients
    new_second = beta_second * moment_second + (1.0 - beta_second) * gradients * gradients
    fix_first = 1.0 - jnp.power(jnp.float32(beta_first), steps)
    fix_second = 1.0 - jnp.power(jnp.float32(beta_second), steps)
    offsets = jnp.cumsum(tensor_rows) - tensor_rows
    first_row = lax.axis_index("dp") * rows_dev
    member = membership(first_row, rows_dev, offsets, tensor_rows)
    mask_rows = jnp.dot(decay_mask.astype(jnp.float32), member, precision=lax.Precision.HIGHEST)
    update = new_first / fix_first / (jnp.sqrt(new_second / fix_second) + adam_epsilon)
    update = update + decay_rate * mask_rows[:, None] * master
    weight_part = jnp.dot(member, jnp.sum(master * master, axis=1), precision=lax.Precision.HIGHEST)
    update_part = jnp.dot(member, jnp.sum(update * update, axis=1), precision=lax.Precision.HIGHEST)
    column_sums = together((weight_part, update_part), "mp")
    weight_sq, update_sq = together((column_sums[0], column_sums[1]), "dp")
    ratio = jnp.sqrt(weight_sq) / (jnp.sqrt(update_sq) + norm_epsilon)
    ratio_rows = jnp.dot(ratio, member, precision=lax.Precision.HIGHEST)
    new_master = master - learn_rate * ratio_rows[:, None] * update
    compute_weights = lax.all_gather(new_master.astype(jnp.bfloat16), "dp", axis=0, tiled=True)
    return (new_master, new_first, new_second, compute_weights)


def solution(mesh):
    placed = (P("dp", "mp"), P("dp", "mp"), P("dp", "mp"), P("dp", "mp"), P(), P(), P())
    return jax.shard_map(
        local,
        mesh=mesh,
        in_specs=placed,
        out_specs=(P("dp", "mp"), P("dp", "mp"), P("dp", "mp"), P(None, "mp")),
        check_vma=False,
    )
```

profile of v0, /device:TPU:1, one launch (start us, length us, event | category | flops | bytes accessed | tf_op | source)
XLA Modules:
  0.0 118.2 jit_solution(8679923997820081381)
XLA Ops:
  7.2 0.0 all-gather.2.cloned.1.call-start
  8.0 0.7 copy.14
  8.7 0.1 reduce.2
  8.9 0.7 sub.18
  9.5 0.1 compare_and_fusion
  9.6 0.8 fusion.2
  10.4 0.0 copy-start
  10.4 5.1 %multiply_reduce_fusion = (f32[512]{0:T(512)S(1)}, f32[512,640]{1,0:T(8,128)S(1)}, f32[512,640]{1,0:T(8,128)}, f32[512,640]{1,0:T(8,128)}, f32[512]{0:T(512)S(1)}) fusion(f32[512,640]{1,0:T(8,128)} %param.7, f32[512]{0:T(512)S(1)} %broadcast_multiply_fusion.1, f32[]{:T(128)} %bitcast.4, f32[]{:T(128)} %bitcast.3, f32[512,640]{1,0:T(8,128)} %param.10, ...), kind=kLoop, calls=%fused_computation.3 | loop fusion | flops 5569536 | bytes 9181192 | tf_op jit(solution)/shard_map/reduce_sum | solution.py:55
  15.5 0.1 convolution_bitcast_fusion
  15.6 0.1 convolution_bitcast_fusion.1
  15.7 0.1 pad_maximum_fusion
  15.8 13.8 %all_to_all.12 = f32[8,1,48]{2,1,0:T(1,128)S(1)} all-to-all(f32[8,1,48]{2,1,0:T(1,128)S(1)} %broadcast_in_dim.4), channel_id=1, replica_groups=mesh['dp'=16,'mp'=8] {'mp'}, dimensions={0} | all-to-all | bytes 3072 | tf_op jit(solution)/shard_map/all_to_all | solution.py:16
  29.7 12.8 %all_to_all.13 = f32[16,1,48]{2,1,0:T(1,128)S(1)} all-to-all(f32[16,1,48]{2,1,0:T(1,128)S(1)} %broadcast_in_dim.5), channel_id=1, replica_groups=mesh['dp'=16,'mp'=8] {'dp'}, dimensions={0} | all-to-all | bytes 6144 | tf_op jit(solution)/shard_map/all_to_all | solution.py:16
  42.5 0.2 fusion.3
  42.7 0.0 copy-done
  42.7 1.5 %fusion.7 = (bf16[512,640]{1,0:T(8,128)(2,1)}, f32[512,640]{1,0:T(8,128)}) fusion(f32[512,640]{1,0:T(8,128)S(1)} %copy-done, f32[512,640]{1,0:T(8,128)S(1)} %get-tuple-element.7, f32[512]{0:T(512)S(1)} %broadcast_multiply_fusion), kind=kLoop, calls=%fused_computation.21 | loop fusion | flops 983040 | bytes 4589568 | tf_op jit(solution)/shard_map/convert_element_type | solution.py:61
  44.2 0.0 all-gather.2.cloned.1.call-update
  44.2 58.2 %all-gather.2.cloned.1.call-done = bf16[8192,640]{1,0:T(8,128)(2,1)} async-done(((bf16[512,640]{1,0:T(8,128)(2,1)}), bf16[8192,640]{1,0:T(8,128)(2,1)}) %all-gather.2.cloned.1.call-update) | async-done | bytes 10485776 | tf_op jit(solution)/shard_map/all_gather | solution.py:61
  102.4 9.0 %copy.19 = bf16[8192,640]{1,0:T(8,128)(2,1)} copy(bf16[8192,640]{1,0:T(8,128)(2,1)} %all-gather.2.cloned.1.call-done) | data formatting | bytes 20971520
  (8 shorter events, 0.1 us)
Async XLA Ops:
  7.2 95.2 %all-gather.2.cloned.1.call-start = ((), (), s32[]{:S(2)}) async-start(), calls=%async_computation.2 | async-start | bytes 11141120 | tf_op jit(solution)/shard_map/all_gather | solution.py:61
  10.4 32.3 %copy-start = (f32[512,640]{1,0:T(8,128)S(1)}, f32[512,640]{1,0:T(8,128)}, u32[]{:S(2)}) copy-start(f32[512,640]{1,0:T(8,128)} %param.7) | copy-start | bytes 3932164
Sparse Core Ops, SparseCore 0:
  44.3 58.0 all-gather.1
where the time goes:
time: 118 us
  waiting for transfers between devices  58.2 us (49%)
  blocking collectives  26.6 us (23%)
  between operations  14.8 us (13%)
  local copies, waits for them, and re-layouts  9.72 us (8%)
  other arithmetic  7.61 us (6%)
  matrix products  1.26 us (1%)
    all_gather x1, waiting for transfers between devices, local(): lax.all_gather(new_master.astype(jnp.bfloat16), 'dp', axis=0, tiled=True)  58.2 us
    all_to_all x2, blocking collectives, copy_for_each(): lax.all_to_all(jnp.broadcast_to(x[None], (size, *x.shape)), axis, 0, 0, t...  26.6 us
    unnamed x3, local copies, waits for them, and re-layouts  8.97 us
    reduce_sum x1, other arithmetic, local(): jnp.sum(update * update, axis=1)  5.08 us
  transfers between devices with their start and end apart: 1, of which 1 were waited for; matrix products, arithmetic and copies ran while one was open for 0% of the time, Pallas kernels for 0%

commit v1 on v0

v1 whole, which is shorter than its diff:
```python
import functools

import jax
import jax.numpy as jnp
from jax import lax
from jax.experimental import pallas as pl
from jax.experimental.pallas import tpu as pltpu
from jax.sharding import PartitionSpec as P

MESH = pl.DeviceIdType.MESH

beta_first = 0.9
beta_second = 0.999
adam_epsilon = 1e-06
decay_rate = 0.3
learn_rate = 0.3
norm_epsilon = 1e-06

TENSORS = 24
ROWS = 512
COLS = 640
DP = 16
MP = 8
REACH = 3
PEERS = (2 * REACH + 1) * MP

LOAD = 64
LOADS = ROWS // LOAD
CH = 32
CHUNKS = ROWS // CH
A = tuple(range(9))
B = tuple(range(9, 16))
UP = frozenset((0, 2, 4, 6, 8, 10, 12, 14))
UP_CROSSED = frozenset((1, 3, 5, 7))


def forwards(kind, k):
    if kind == "up1":
        return (("up", "z2"),) * (k in UP) + (("x", "x_up"),) * (k in B)
    if kind == "down1":
        return (("down", "z2"),) * (k not in UP) + (("x", "x_down"),) * (k in B)
    if kind == "z2":
        return (("x", "x_z2"),) * (k in B)
    if kind == "x0":
        return (("up", "x_up"), ("down", "x_down")) if k in A else ()
    if kind == "x_up" and k in A:
        return (("up", "x_z2"),) * (k in UP_CROSSED)
    if kind == "x_down" and k in A:
        return (("down", "x_z2"),) * (k not in UP_CROSSED)
    return ()


def own_order():
    order = []
    for i in range(len(A)):
        order.append((A[i], "x"))
        if i < len(B):
            order += [(B[i], "up"), (B[i], "down")]
    for i in range(len(A)):
        order += [(A[i], "up"), (A[i], "down")]
        if i < len(B):
            order.append((B[i], "x"))
    return order


def arrival_order():
    first = {"up": "up1", "down": "down1", "x": "x0"}
    free = {"up": 0.0, "down": 0.0, "x": 0.0}
    pending, order = [], []

    def send(link, kind, k, now):
        free[link] = max(free[link], now) + 0.88
        pending.append((free[link] + 2.0, len(pending) + len(order), kind, k))

    for k, link in own_order():
        send(link, first[link], k, 0.0)
    while pending:
        pending.sort()
        now, _, kind, k = pending.pop(0)
        order.append((kind, k))
        for link, there in forwards(kind, k):
            send(link, there, k, now)
    return order


ORDER = arrival_order()
SLOT = {item: n for n, item in enumerate(ORDER)}


def kernel(steps_ref, rows_hbm, decay_hbm, master_hbm, first_hbm, second_hbm, grad_hbm,
           master_out, first_out, second_out, weights,
           master, first, second, grad, update, decay_rows, part, parts, rows_ref, decay_ref, small_sem,
           load_sem, part_send, part_recv, up_send, down_send, x_send, core_send, recv_sem, core_recv):
    d, m = lax.axis_index("dp"), lax.axis_index("mp")
    z, x, c = d // 4, (d // 2) % 2, d % 2
    step = 1 + 2 * c
    z_up, z_down, z_far = (z + step) % 4, (z + 4 - step) % 4, (z + 2) % 4

    def device(zz, xx, cc):
        return (zz * 2 + xx) * 2 + cc

    target = {"up": device(z_up, x, c), "down": device(z_down, x, c), "x": device(z, 1 - x, c)}
    partner = device(z, x, 1 - c)
    send_sem = {"up": up_send, "down": down_send, "x": x_send}

    peers = []
    for reach in range(-REACH, REACH + 1):
        for hi in range(2):
            for y in range(4):
                if (reach, hi, y) != (0, 0, 0):
                    peers.append((-(2 * hi + min(y, 4 - y) + (abs(reach) + 1) // 2), reach, hi, y))
    peers = [
        ((d + DP + reach) % DP, (m // 4 + hi) % 2 * 4 + (m + y) % 4, reach)
        for _, reach, hi, y in sorted(peers)
    ]

    smalls = [
        pltpu.make_async_copy(src, dst, small_sem.at[n])
        for n, (src, dst) in enumerate(((rows_hbm, rows_ref), (decay_hbm, decay_ref)))
    ]
    for one in smalls:
        one.start()
    for n in range(LOADS):
        span = pl.ds(n * LOAD, LOAD)
        for a, (src, dst) in enumerate(
            ((master_hbm, master), (first_hbm, first), (second_hbm, second), (grad_hbm, grad))
        ):
            pltpu.make_async_copy(src.at[span], dst.at[span], load_sem.at[n, a]).start()

    barrier = pltpu.get_barrier_semaphore()
    for pd, pm, _ in peers:
        pl.semaphore_signal(barrier, inc=1, device_id=(pd, pm), device_id_type=MESH)
    for link in ("up", "down"):
        pl.semaphore_signal(barrier, inc=1, device_id=(target[link], m), device_id_type=MESH)

    lane = lax.broadcasted_iota(jnp.int32, (8, 128), 1)
    sub = lax.broadcasted_iota(jnp.int32, (8, 128), 0)
    for one in smalls:
        one.wait()
    start = jnp.zeros((8, 128), jnp.int32)
    end = jnp.zeros((8, 128), jnp.int32)
    decay = jnp.zeros((8, 128), jnp.float32)
    offset = jnp.int32(0)
    for t in range(TENSORS):
        here = lane % 32 == t
        after = offset + rows_ref[t]
        start = jnp.where(here, offset, start)
        end = jnp.where(here, after, end)
        decay = jnp.where(here, decay_ref[t].astype(jnp.float32) * decay_rate, decay)
        offset = after
    decay = jnp.where(lane < 32, decay, 0.0)

    steps = jnp.full((8, 128), steps_ref[0], jnp.int32)
    power_first = jnp.ones((8, 128), jnp.float32)
    power_second = jnp.ones((8, 128), jnp.float32)
    base_first, base_second = jnp.float32(beta_first), jnp.float32(beta_second)
    base_first = jnp.full((8, 128), base_first)
    base_second = jnp.full((8, 128), base_second)
    for _ in range(31):
        odd = steps % 2 == 1
        power_first = jnp.where(odd, power_first * base_first, power_first)
        power_second = jnp.where(odd, power_second * base_second, power_second)
        base_first, base_second, steps = base_first * base_first, base_second * base_second, steps // 2
    inv_first = (1.0 / (1.0 - power_first))[:, :1]
    inv_second = (1.0 / (1.0 - power_second))[:, :1]

    first_row = d * ROWS

    def member(row):
        ids = sub + (first_row + row)
        return (ids >= start) & (ids < end)

    def decay_step(n, carry):
        for g in range(8):
            row = n * 64 + g * 8
            value = jnp.sum(jnp.where(member(row), decay, 0.0), axis=1, keepdims=True)
            decay_rows[pl.ds(pl.multiple_of(row, 8), 8), :] = jnp.broadcast_to(value, (8, 128))
        return carry

    lax.fori_loop(0, ROWS // 64, decay_step, 0)

    def load_step(n, total):
        span = pl.ds(pl.multiple_of(n * LOAD, LOAD), LOAD)
        for a, (src, dst) in enumerate(
            ((master_hbm, master), (first_hbm, first), (second_hbm, second), (grad_hbm, grad))
        ):
            pltpu.make_async_copy(src.at[span], dst.at[span], load_sem.at[n, a]).wait()
        for g in range(LOAD // 8):
            row = n * LOAD + g * 8
            here = pl.ds(pl.multiple_of(row, 8), 8)
            w, gr = master[here, :], grad[here, :]
            new_first = beta_first * first[here, :] + (1.0 - beta_first) * gr
            new_second = beta_second * second[here, :] + (1.0 - beta_second) * gr * gr
            first_out[here, :] = new_first
            second_out[here, :] = new_second
            up = (new_first * inv_first) / (jnp.sqrt(new_second * inv_second) + adam_epsilon)
            up = up + decay_rows[here, :][:, :1] * w
            update[here, :] = up
            w_sum = jnp.sum(w * w, axis=1, keepdims=True)
            u_sum = jnp.sum(up * up, axis=1, keepdims=True)
            total = total + jnp.where(member(row), jnp.where(lane < 32, w_sum, u_sum), 0.0)
        return total

    total = lax.fori_loop(0, LOADS, load_step, jnp.zeros((8, 128), jnp.float32))
    total = jnp.sum(total, axis=0, keepdims=True)
    part[...] = total
    parts[REACH * MP + m] = total

    pl.semaphore_wait(barrier, len(peers) + 2)
    for pd, pm, reach in peers:
        pltpu.make_async_remote_copy(
            src_ref=part, dst_ref=parts.at[(reach + REACH) * MP + m], send_sem=part_send, recv_sem=part_recv,
            device_id=(pd, pm), device_id_type=MESH,
        ).start()
    others = parts.at[pl.ds(0, PEERS - 1)]
    pltpu.make_async_copy(others, others, part_recv).wait()

    sums = jnp.sum(parts[...], axis=0)
    sums = jnp.broadcast_to(sums, (8, 128))
    u_sq = pltpu.roll(sums, 96, 1)
    ratio = learn_rate * (jnp.sqrt(sums) / (jnp.sqrt(u_sq) + norm_epsilon))
    ratio = jnp.where(lane < TENSORS, ratio, 0.0)

    def chunk(dev, k):
        return weights.at[pl.ds(pl.multiple_of(dev * ROWS + k * CH, CH), CH)]

    def copy(link, kind, dev, k):
        return pltpu.make_async_remote_copy(
            src_ref=chunk(dev, k), dst_ref=chunk(dev, k), send_sem=send_sem[link], recv_sem=recv_sem.at[SLOT[kind, k]],
            device_id=(target[link], m), device_id_type=MESH,
        )

    def share(dev, k):
        pltpu.make_async_remote_copy(
            src_ref=chunk(dev, k), dst_ref=chunk(dev, k), send_sem=core_send, recv_sem=core_recv,
            device_id=(partner, m), device_id_type=MESH,
        ).start()

    def finish(k):
        for g in range(CH // 16):
            halves = []
            for h in range(2):
                row = k * CH + g * 16 + h * 8
                scale = jnp.sum(jnp.where(member(row), ratio, 0.0), axis=1, keepdims=True)
                halves.append(master[pl.ds(row, 8), :] - scale * update[pl.ds(row, 8), :])
            value = jnp.concatenate(halves, axis=0)
            row = k * CH + g * 16
            master_out[pl.ds(row, 16), :] = value
            weights[pl.ds(pl.multiple_of(d * ROWS + row, 16), 16), :] = value.astype(jnp.bfloat16)

    first_kind = {"up": "up1", "down": "down1", "x": "x0"}
    done = set()
    for k, link in own_order():
        if k not in done:
            finish(k)
        copy(link, first_kind[link], d, k).start()
        if k not in done:
            share(d, k)
            done.add(k)

    origin = {
        "up1": device(z_down, x, c), "down1": device(z_up, x, c), "z2": device(z_far, x, c),
        "x0": device(z, 1 - x, c), "x_up": device(z_down, 1 - x, c), "x_down": device(z_up, 1 - x, c),
        "x_z2": device(z_far, 1 - x, c),
    }
    sent = {"up": CHUNKS, "down": CHUNKS, "x": CHUNKS}
    for kind, k in ORDER:
        dev = origin[kind]
        copy("x", kind, dev, k).wait_recv()
        for link, there in forwards(kind, k):
            copy(link, there, dev, k).start()
            sent[link] += 1
        share(dev, k)

    def rows_of(count):
        return weights.at[pl.ds(0, count * CH)]

    pltpu.make_async_copy(rows_of(8 * CHUNKS), rows_of(8 * CHUNKS), core_recv).wait()
    pltpu.make_async_copy(rows_of(8 * CHUNKS), rows_of(8 * CHUNKS), core_send).wait()
    for link, count in sent.items():
        pltpu.make_async_copy(rows_of(count), rows_of(count), send_sem[link]).wait()
    pltpu.make_async_copy(others, others, part_send).wait()


def store_kernel(*refs):
    sources, sinks, sem = refs[:4], refs[4:8], refs[8]
    copies = []
    for n, (src, dst) in enumerate(zip(sources, sinks)):
        pieces = 8 if n == 3 else 1
        rows = src.shape[0] // pieces
        for i in range(pieces):
            span = pl.ds(i * rows, rows)
            copies.append(pltpu.make_async_copy(src.at[span], dst.at[span], sem.at[len(copies)]))
    for one in copies:
        one.start()
    for one in copies:
        one.wait()


def local(master, moment_first, moment_second, gradients, step_count, tensor_rows, decay_mask):
    hbm = pl.BlockSpec(memory_space=pltpu.MemorySpace.HBM)
    vmem = pl.BlockSpec(memory_space=pltpu.MemorySpace.VMEM)
    smem = pl.BlockSpec(memory_space=pltpu.MemorySpace.SMEM)
    f32 = jnp.float32
    block = (ROWS, COLS)
    results = pl.pallas_call(
        kernel,
        name="lamb_gather",
        out_shape=[pltpu.VMEM(block, f32)] * 3 + [pltpu.VMEM((DP * ROWS, COLS), jnp.bfloat16)],
        in_specs=[smem] + [hbm] * 6,
        out_specs=[vmem] * 4,
        scratch_shapes=[pltpu.VMEM(block, f32)] * 5 + [
            pltpu.VMEM((ROWS, 128), f32),
            pltpu.VMEM((1, 128), f32),
            pltpu.VMEM((PEERS, 1, 128), f32),
            pltpu.SMEM((TENSORS,), jnp.int32),
            pltpu.SMEM((TENSORS,), jnp.int32),
            pltpu.SemaphoreType.DMA((2,)),
            pltpu.SemaphoreType.DMA((LOADS, 4)),
        ] + [pltpu.SemaphoreType.DMA] * 6 + [
            pltpu.SemaphoreType.DMA((len(ORDER),)),
            pltpu.SemaphoreType.DMA,
        ],
        compiler_params=pltpu.CompilerParams(collective_id=0, has_side_effects=True, vmem_limit_bytes=49 << 20),
    )(step_count, *[
        pltpu.with_memory_space_constraint(x, pltpu.MemorySpace.HBM)
        for x in (tensor_rows, decay_mask, master, moment_first, moment_second, gradients)
    ])
    return pl.pallas_call(
        store_kernel,
        name="store",
        out_shape=[jax.ShapeDtypeStruct(block, f32)] * 3 + [jax.ShapeDtypeStruct((DP * ROWS, COLS), jnp.bfloat16)],
        in_specs=[vmem] * 4,
        out_specs=[hbm] * 4,
        scratch_shapes=[pltpu.SemaphoreType.DMA((11,))],
        compiler_params=pltpu.CompilerParams(vmem_limit_bytes=4 << 20),
    )(*results)


def solution(mesh):
    placed = (P("dp", "mp"), P("dp", "mp"), P("dp", "mp"), P("dp", "mp"), P(), P(), P())
    return jax.shard_map(
        local,
        mesh=mesh,
        in_specs=placed,
        out_specs=(P("dp", "mp"), P("dp", "mp"), P("dp", "mp"), P(None, "mp")),
        check_vma=False,
    )
```

time: 118 us -> 59.9 us (0.51)
  Pallas kernels: 0 us -> 58.5 us
  waiting for transfers between devices: 58.2 us -> 0 us
  blocking collectives: 26.6 us -> 0 us
  between operations: 14.8 us -> 1.29 us
  local copies, waits for them, and re-layouts: 9.72 us -> 0 us
  other arithmetic: 7.61 us -> 0 us
  matrix products: 1.26 us -> 0 us
    pallas_call x0 -> x2, Pallas kernels: none -> 58.5 us  [the longest x1 53.3 us: local(): pl.pallas_call(kernel, name='lamb_gather', out_shape=[pltpu.VMEM(block, f...]
    all_gather x1 -> x0, waiting for transfers between devices: 58.2 us -> none  [local(): lax.all_gather(new_master.astype(jnp.bfloat16), 'dp', axis=0, tiled=True)]
    all_to_all x2 -> x0, blocking collectives: 26.6 us -> none  [copy_for_each(): lax.all_to_all(jnp.broadcast_to(x[None], (size, *x.shape)), axis, 0, 0, t...]
    unnamed x3 -> x0, local copies, waits for them, and re-layouts: 8.97 us -> none
    reduce_sum x3 -> x0, other arithmetic: 5.12 us -> none  [the longest x1 5.08 us: local(): jnp.sum(update * update, axis=1)]
    convert_element_type x1 -> x0, other arithmetic: 1.49 us -> none  [local(): new_master.astype(jnp.bfloat16)]
    dot_general x4 -> x0, matrix products: 1.26 us -> none  [the longest x1 0.79 us: local(): jnp.dot(decay_mask.astype(jnp.float32), member, precision=lax.Precision.H...]
  transfers between devices with their start and end apart: 1 -> 0, of which waited for: 1 -> 0; matrix products, arithmetic and copies ran while one was open for 0% -> 0% of each run, Pallas kernels for 0% -> 0%
where the time goes in v1:
time: 59.9 us; the launch traced here: 59.8 us
  Pallas kernels  58.5 us (98%)
  between operations  1.29 us (2%)
    pallas_call x1, Pallas kernels, local(): pl.pallas_call(kernel, name='lamb_gather', out_shape=[pltpu.VMEM(block, f...  53.3 us
    pallas_call x1, Pallas kernels, local(): pl.pallas_call(store_kernel, name='store', out_shape=[jax.ShapeDtypeStruc...  5.24 us

profile of v1, /device:TPU:1, one launch (start us, length us, event | category | flops | bytes accessed | tf_op | source)
XLA Modules:
  0.0 59.8 jit_solution(98245222791548690)
XLA Ops:
  1.3 53.3 %lamb_gather.1 = (f32[512,640]{1,0:T(8,128)S(1)}, f32[512,640]{1,0:T(8,128)S(1)}, f32[512,640]{1,0:T(8,128)S(1)}, bf16[8192,640]{1,0:T(8,128)(2,1)S(1)}) custom-call(s32[1]{0:T(128)S(6)} %copy.11.steps_ref, s32[24]{0:T(128)} %rows_hbm.1, s32[24]{0:T(128)} %decay_hbm.1, f32[512,640]{1,0:T(8,128)} %master_hbm.1, f32[512,640]{1,0:T(8,128)} %first_hbm.1, ...), custom_call_target="tpu_custom_call" | custom-call | tf_op jit(solution)/shard_map/lamb_gather/pallas_call | solution.py:306
  54.6 5.2 %store.1 = (f32[512,640]{1,0:T(8,128)}, f32[512,640]{1,0:T(8,128)}, f32[512,640]{1,0:T(8,128)}, bf16[8192,640]{1,0:T(8,128)(2,1)}) custom-call(f32[512,640]{1,0:T(8,128)S(1)} %get-tuple-element.8.refs_0_, f32[512,640]{1,0:T(8,128)S(1)} %get-tuple-element.9.refs_1_, f32[512,640]{1,0:T(8,128)S(1)} %get-tuple-element.10.refs_2_, ...), custom_call_target="tpu_custom_call" | custom-call | tf_op jit(solution)/shard_map/store/pallas_call | solution.py:329

commit v2 on v1

v2 whole, which is shorter than its diff:
```python
import functools

import jax
import jax.numpy as jnp
from jax import lax
from jax.experimental import pallas as pl
from jax.experimental.pallas import tpu as pltpu
from jax.sharding import PartitionSpec as P

MESH = pl.DeviceIdType.MESH

beta_first = 0.9
beta_second = 0.999
adam_epsilon = 1e-06
decay_rate = 0.3
learn_rate = 0.3
norm_epsilon = 1e-06

TENSORS = 24
ROWS = 512
COLS = 640
DP = 16
MP = 8
REACH = 3
PEERS = (2 * REACH + 1) * MP

LOAD = 64
LOADS = ROWS // LOAD
PIECE = 32
CHUNKS = (96, 96, 96, 112, 112)
STARTS = tuple(sum(CHUNKS[:k]) for k in range(len(CHUNKS)))
A = (0, 1, 2)
B = (3, 4)
UP = frozenset((0, 2, 3))
UP_CROSSED = frozenset((1,))


def forwards(kind, k):
    if kind == "up1":
        return (("up", "z2"),) * (k in UP) + (("x", "x_up"),) * (k in B)
    if kind == "down1":
        return (("down", "z2"),) * (k not in UP) + (("x", "x_down"),) * (k in B)
    if kind == "z2":
        return (("x", "x_z2"),) * (k in B)
    if kind == "x0":
        return (("up", "x_up"), ("down", "x_down")) if k in A else ()
    if kind == "x_up" and k in A:
        return (("up", "x_z2"),) * (k in UP_CROSSED)
    if kind == "x_down" and k in A:
        return (("down", "x_z2"),) * (k not in UP_CROSSED)
    return ()


def own_order():
    first = [(A[0], "x"), (B[0], "up"), (B[0], "down"), (A[1], "x"), (B[1], "up"), (B[1], "down"), (A[2], "x")]
    return first, [(k, link) for k in A for link in ("up", "down")] + [(k, "x") for k in B]


def arrival_order():
    first = {"up": "up1", "down": "down1", "x": "x0"}
    free = {"up": 0.0, "down": 0.0, "x": 0.0}
    pending, order = [], []

    def send(link, kind, k, now):
        free[link] = max(free[link], now) + CHUNKS[k] / 36.4
        pending.append((free[link] + 2.0, len(pending) + len(order), kind, k))

    for k, link in sum(own_order(), []):
        send(link, first[link], k, 0.0)
    while pending:
        pending.sort()
        now, _, kind, k = pending.pop(0)
        order.append((kind, k))
        for link, there in forwards(kind, k):
            send(link, there, k, now)
    return order


ORDER = arrival_order()
SLOT = {item: n for n, item in enumerate(ORDER)}


def kernel(steps_ref, rows_hbm, decay_hbm, master_hbm, first_hbm, second_hbm, grad_hbm,
           master_out, first_out, second_out, weights,
           master, first, second, grad, update, part, parts, rows_ref, decay_ref, small_sem,
           load_sem, part_send, part_recv, up_send, down_send, x_send, core_send, recv_sem, core_recv):
    d, m = lax.axis_index("dp"), lax.axis_index("mp")
    z, x, c = d // 4, (d // 2) % 2, d % 2
    step = 1 + 2 * c
    z_up, z_down, z_far = (z + step) % 4, (z + 4 - step) % 4, (z + 2) % 4

    def device(zz, xx, cc):
        return (zz * 2 + xx) * 2 + cc

    target = {"up": device(z_up, x, c), "down": device(z_down, x, c), "x": device(z, 1 - x, c)}
    partner = device(z, x, 1 - c)
    send_sem = {"up": up_send, "down": down_send, "x": x_send}

    reaches = sorted(range(-REACH, REACH + 1), key=lambda r: -abs(r))
    others = sorted(((hi, y) for hi in range(2) for y in range(4)), key=lambda p: -(2 * p[0] + min(p[1], 4 - p[1])))

    def inside(reach):
        return (d + reach >= 0) & (d + reach < DP)

    def peers(reach):
        return [
            (d + reach, (m // 4 + hi) % 2 * 4 + (m + y) % 4) for hi, y in others if (reach, hi, y) != (0, 0, 0)
        ]

    def from_reach(reach):
        return parts.at[pl.ds((reach + REACH) * MP, MP - (reach == 0))]

    smalls = [
        pltpu.make_async_copy(src, dst, small_sem.at[n])
        for n, (src, dst) in enumerate(((rows_hbm, rows_ref), (decay_hbm, decay_ref)))
    ]
    for one in smalls:
        one.start()
    for n in range(LOADS):
        span = pl.ds(n * LOAD, LOAD)
        for src, dst in ((master_hbm, master), (first_hbm, first), (second_hbm, second), (grad_hbm, grad)):
            pltpu.make_async_copy(src.at[span], dst.at[span], load_sem.at[n]).start()

    parts[...] = jnp.zeros((PEERS, 1, 128), jnp.float32)
    barrier = pltpu.get_barrier_semaphore()
    for reach in reaches:
        @pl.when(inside(reach))
        def _():
            for pd, pm in peers(reach):
                pl.semaphore_signal(barrier, inc=1, device_id=(pd, pm), device_id_type=MESH)
    for link in ("up", "down"):
        pl.semaphore_signal(barrier, inc=1, device_id=(target[link], m), device_id_type=MESH)

    steps = jnp.full((8, 128), steps_ref[0], jnp.int32)
    power_first = jnp.ones((8, 128), jnp.float32)
    power_second = jnp.ones((8, 128), jnp.float32)
    base_first, base_second = jnp.float32(beta_first), jnp.float32(beta_second)
    base_first = jnp.full((8, 128), base_first)
    base_second = jnp.full((8, 128), base_second)
    for _ in range(31):
        odd = steps % 2 == 1
        power_first = jnp.where(odd, power_first * base_first, power_first)
        power_second = jnp.where(odd, power_second * base_second, power_second)
        base_first, base_second, steps = base_first * base_first, base_second * base_second, steps // 2
    fix_first = 1.0 - power_first
    den_scale = (fix_first * jnp.sqrt(1.0 / (1.0 - power_second)))[:1, :1]
    den_shift = (fix_first * adam_epsilon)[:1, :1]

    lane = lax.broadcasted_iota(jnp.int32, (8, 128), 1)
    sub = lax.broadcasted_iota(jnp.int32, (8, 128), 0)
    for one in smalls:
        one.wait()
    start = jnp.zeros((8, 128), jnp.int32)
    end = jnp.zeros((8, 128), jnp.int32)
    decay = jnp.zeros((8, 128), jnp.float32)
    offset = jnp.int32(0)
    for t in range(TENSORS):
        here = lane % 32 == t
        after = offset + rows_ref[t]
        start = jnp.where(here, offset, start)
        end = jnp.where(here, after, end)
        decay = jnp.where(here, decay_ref[t].astype(jnp.float32) * decay_rate, decay)
        offset = after
    decay = jnp.where(lane < 32, decay, 0.0)

    first_row = d * ROWS

    def member(row):
        ids = sub + (first_row + row)
        return (ids >= start) & (ids < end)

    def load_step(n, total):
        four = master.at[pl.ds(0, 4 * LOAD)]
        pltpu.make_async_copy(four, four, load_sem.at[n]).wait()
        for g in range(LOAD // 8):
            row = n * LOAD + g * 8
            here = pl.ds(pl.multiple_of(row, 8), 8)
            w, gr = master[here, :], grad[here, :]
            new_first = beta_first * first[here, :] + (1.0 - beta_first) * gr
            new_second = beta_second * second[here, :] + (1.0 - beta_second) * gr * gr
            first_out[here, :] = new_first
            second_out[here, :] = new_second
            owned = member(row)
            decay_row = jnp.sum(jnp.where(owned, decay, 0.0), axis=1, keepdims=True)
            up = new_first / (jnp.sqrt(new_second) * den_scale + den_shift) + decay_row * w
            update[here, :] = up
            w_sum = jnp.sum(w * w, axis=1, keepdims=True)
            u_sum = jnp.sum(up * up, axis=1, keepdims=True)
            total = total + jnp.where(owned, jnp.where(lane < 32, w_sum, u_sum), 0.0)
        return total

    total = lax.fori_loop(0, LOADS, load_step, jnp.zeros((8, 128), jnp.float32))
    total = jnp.sum(total, axis=0, keepdims=True)
    part[...] = total
    parts[REACH * MP + m] = total

    blocks = sum(inside(reach).astype(jnp.int32) for reach in reaches)
    pl.semaphore_wait(barrier, blocks * MP + 1)

    for reach in reaches:
        @pl.when(inside(reach))
        def _():
            for pd, pm in peers(reach):
                pltpu.make_async_remote_copy(
                    src_ref=part, dst_ref=parts.at[(REACH - reach) * MP + m],
                    send_sem=part_send.at[REACH - reach], recv_sem=part_recv.at[REACH - reach],
                    device_id=(pd, pm), device_id_type=MESH,
                ).start()

    def drain(sem):
        for reach in reaches:
            @pl.when(inside(reach))
            def _():
                pltpu.make_async_copy(from_reach(reach), from_reach(reach), sem(reach)).wait()

    drain(lambda reach: part_recv.at[REACH + reach])

    sums = jnp.sum(parts[...], axis=0)
    sums = jnp.broadcast_to(sums, (8, 128))
    u_sq = pltpu.roll(sums, 96, 1)
    ratio = learn_rate * (jnp.sqrt(sums) / (jnp.sqrt(u_sq) + norm_epsilon))
    ratio = jnp.where(lane < TENSORS, ratio, 0.0)

    def copy(link, kind, dev, k, part_of=None):
        row, rows = part_of or (STARTS[k], CHUNKS[k])
        span = weights.at[pl.ds(pl.multiple_of(dev * ROWS + row, 16), rows)]
        return pltpu.make_async_remote_copy(
            src_ref=span, dst_ref=span, send_sem=send_sem[link], recv_sem=recv_sem.at[SLOT[kind, k]],
            device_id=(target[link], m), device_id_type=MESH,
        )

    def share(dev, row, rows):
        span = weights.at[pl.ds(pl.multiple_of(dev * ROWS + row, 16), rows)]
        pltpu.make_async_remote_copy(
            src_ref=span, dst_ref=span, send_sem=core_send, recv_sem=core_recv,
            device_id=(partner, m), device_id_type=MESH,
        ).start()

    def finish(first_of, rows):
        for row in range(first_of, first_of + rows, 16):
            halves = []
            for h in (row, row + 8):
                scale = jnp.sum(jnp.where(member(h), ratio, 0.0), axis=1, keepdims=True)
                halves.append(master[pl.ds(h, 8), :] - scale * update[pl.ds(h, 8), :])
            value = jnp.concatenate(halves, axis=0)
            master_out[pl.ds(row, 16), :] = value
            weights[pl.ds(pl.multiple_of(d * ROWS + row, 16), 16), :] = value.astype(jnp.bfloat16)

    first_kind = {"up": "up1", "down": "down1", "x": "x0"}
    pieces = {
        group: [
            (k, STARTS[k] + at, min(PIECE, CHUNKS[k] - at)) for k in group for at in range(0, CHUNKS[k], PIECE)
        ]
        for group in (A, B)
    }
    for turn in range(len(pieces[A])):
        for group, links in ((A, ("x",)), (B, ("up", "down"))):
            if turn < len(pieces[group]):
                k, row, rows = pieces[group][turn]
                finish(row, rows)
                for link in links:
                    copy(link, first_kind[link], d, k, (row, rows)).start()
                share(d, row, rows)
    for k, link in own_order()[1]:
        copy(link, first_kind[link], d, k).start()

    origin = {
        "up1": device(z_down, x, c), "down1": device(z_up, x, c), "z2": device(z_far, x, c),
        "x0": device(z, 1 - x, c), "x_up": device(z_down, 1 - x, c), "x_down": device(z_up, 1 - x, c),
        "x_z2": device(z_far, 1 - x, c),
    }
    sent = {"up": ROWS, "down": ROWS, "x": ROWS}
    for kind, k in ORDER:
        dev = origin[kind]
        copy("x", kind, dev, k).wait_recv()
        for link, there in forwards(kind, k):
            copy(link, there, dev, k).start()
            sent[link] += CHUNKS[k]
        share(dev, STARTS[k], CHUNKS[k])

    def rows_of(count):
        return weights.at[pl.ds(0, count)]

    pltpu.make_async_copy(rows_of(8 * ROWS), rows_of(8 * ROWS), core_recv).wait()
    pltpu.make_async_copy(rows_of(8 * ROWS), rows_of(8 * ROWS), core_send).wait()
    for link, count in sent.items():
        pltpu.make_async_copy(rows_of(count), rows_of(count), send_sem[link]).wait()
    drain(lambda reach: part_send.at[REACH - reach])


def store_kernel(*refs):
    sources, sinks, sem = refs[:4], refs[4:8], refs[8]
    copies = []
    for n, (src, dst) in enumerate(zip(sources, sinks)):
        pieces = 8 if n == 3 else 1
        rows = src.shape[0] // pieces
        for i in range(pieces):
            span = pl.ds(i * rows, rows)
            copies.append(pltpu.make_async_copy(src.at[span], dst.at[span], sem.at[len(copies)]))
    for one in copies:
        one.start()
    for one in copies:
        one.wait()


def local(master, moment_first, moment_second, gradients, step_count, tensor_rows, decay_mask):
    hbm = pl.BlockSpec(memory_space=pltpu.MemorySpace.HBM)
    vmem = pl.BlockSpec(memory_space=pltpu.MemorySpace.VMEM)
    smem = pl.BlockSpec(memory_space=pltpu.MemorySpace.SMEM)
    f32 = jnp.float32
    block = (ROWS, COLS)
    results = pl.pallas_call(
        kernel,
        name="lamb_gather",
        out_shape=[pltpu.VMEM(block, f32)] * 3 + [pltpu.VMEM((DP * ROWS, COLS), jnp.bfloat16)],
        in_specs=[smem] + [hbm] * 6,
        out_specs=[vmem] * 4,
        scratch_shapes=[pltpu.VMEM(block, f32)] * 5 + [
            pltpu.VMEM((1, 128), f32),
            pltpu.VMEM((PEERS, 1, 128), f32),
            pltpu.SMEM((TENSORS,), jnp.int32),
            pltpu.SMEM((TENSORS,), jnp.int32),
            pltpu.SemaphoreType.DMA((2,)),
            pltpu.SemaphoreType.DMA((LOADS,)),
            pltpu.SemaphoreType.DMA((2 * REACH + 1,)),
            pltpu.SemaphoreType.DMA((2 * REACH + 1,)),
        ] + [pltpu.SemaphoreType.DMA] * 4 + [
            pltpu.SemaphoreType.DMA((len(ORDER),)),
            pltpu.SemaphoreType.DMA,
        ],
        compiler_params=pltpu.CompilerParams(collective_id=0, has_side_effects=True, vmem_limit_bytes=49 << 20),
    )(step_count, *[
        pltpu.with_memory_space_constraint(x, pltpu.MemorySpace.HBM)
        for x in (tensor_rows, decay_mask, master, moment_first, moment_second, gradients)
    ])
    return pl.pallas_call(
        store_kernel,
        name="store",
        out_shape=[jax.ShapeDtypeStruct(block, f32)] * 3 + [jax.ShapeDtypeStruct((DP * ROWS, COLS), jnp.bfloat16)],
        in_specs=[vmem] * 4,
        out_specs=[hbm] * 4,
        scratch_shapes=[pltpu.SemaphoreType.DMA((11,))],
        compiler_params=pltpu.CompilerParams(vmem_limit_bytes=4 << 20),
    )(*results)


def solution(mesh):
    placed = (P("dp", "mp"), P("dp", "mp"), P("dp", "mp"), P("dp", "mp"), P(), P(), P())
    return jax.shard_map(
        local,
        mesh=mesh,
        in_specs=placed,
        out_specs=(P("dp", "mp"), P("dp", "mp"), P("dp", "mp"), P(None, "mp")),
        check_vma=False,
    )
```

time: 59.9 us -> 58.2 us (0.972)
  Pallas kernels: 58.5 us -> 56.8 us
    pallas_call x1, Pallas kernels: 53.3 us -> 51.6 us  [local(): pl.pallas_call(kernel, name='lamb_gather', out_shape=[pltpu.VMEM(block, f...]
where the time goes in v2:
time: 58.2 us; the launch traced here: 58.1 us
  Pallas kernels  56.8 us (98%)
  between operations  1.29 us (2%)
    pallas_call x1, Pallas kernels, local(): pl.pallas_call(kernel, name='lamb_gather', out_shape=[pltpu.VMEM(block, f...  51.6 us
    pallas_call x1, Pallas kernels, local(): pl.pallas_call(store_kernel, name='store', out_shape=[jax.ShapeDtypeStruc...  5.24 us

profile of v2, /device:TPU:1, one launch (start us, length us, event | category | flops | bytes accessed | tf_op | source)
XLA Modules:
  0.0 58.1 jit_solution(9949835686227582750)
XLA Ops:
  1.3 51.6 %lamb_gather.1 = (f32[512,640]{1,0:T(8,128)S(1)}, f32[512,640]{1,0:T(8,128)S(1)}, f32[512,640]{1,0:T(8,128)S(1)}, bf16[8192,640]{1,0:T(8,128)(2,1)S(1)}) custom-call(s32[1]{0:T(128)S(6)} %copy.11.steps_ref, s32[24]{0:T(128)} %rows_hbm.1, s32[24]{0:T(128)} %decay_hbm.1, f32[512,640]{1,0:T(8,128)} %master_hbm.1, f32[512,640]{1,0:T(8,128)} %first_hbm.1, ...), custom_call_target="tpu_custom_call" | custom-call | tf_op jit(solution)/shard_map/lamb_gather/pallas_call | solution.py:312
  52.9 5.2 %store.1 = (f32[512,640]{1,0:T(8,128)}, f32[512,640]{1,0:T(8,128)}, f32[512,640]{1,0:T(8,128)}, bf16[8192,640]{1,0:T(8,128)(2,1)}) custom-call(f32[512,640]{1,0:T(8,128)S(1)} %get-tuple-element.8.refs_0_, f32[512,640]{1,0:T(8,128)S(1)} %get-tuple-element.9.refs_1_, f32[512,640]{1,0:T(8,128)S(1)} %get-tuple-element.10.refs_2_, ...), custom_call_target="tpu_custom_call" | custom-call | tf_op jit(solution)/shard_map/store/pallas_call | solution.py:336

commit v3 on v2

--- a/solution.py
+++ b/solution.py
@@ -27,11 +27,11 @@
 LOAD = 64
 LOADS = ROWS // LOAD
 PIECE = 32
-CHUNKS = (96, 96, 96, 112, 112)
+CHUNKS = (96, 80, 96, 128, 112)
 STARTS = tuple(sum(CHUNKS[:k]) for k in range(len(CHUNKS)))
 A = (0, 1, 2)
 B = (3, 4)
-UP = frozenset((0, 2, 3))
+UP = frozenset((0, 1, 4))
 UP_CROSSED = frozenset((1,))
 
 
@@ -86,8 +86,7 @@
            load_sem, part_send, part_recv, up_send, down_send, x_send, core_send, recv_sem, core_recv):
     d, m = lax.axis_index("dp"), lax.axis_index("mp")
     z, x, c = d // 4, (d // 2) % 2, d % 2
-    step = 1 + 2 * c
-    z_up, z_down, z_far = (z + step) % 4, (z + 4 - step) % 4, (z + 2) % 4
+    z_up, z_down, z_far = (z + 1) % 4, (z + 3) % 4, (z + 2) % 4
 
     def device(zz, xx, cc):
         return (zz * 2 + xx) * 2 + cc
@@ -96,16 +95,18 @@
     partner = device(z, x, 1 - c)
     send_sem = {"up": up_send, "down": down_send, "x": x_send}
 
-    reaches = sorted(range(-REACH, REACH + 1), key=lambda r: -abs(r))
-    others = sorted(((hi, y) for hi in range(2) for y in range(4)), key=lambda p: -(2 * p[0] + min(p[1], 4 - p[1])))
+    columns = sorted(((hi, y) for hi in range(2) for y in range(4)), key=lambda p: -(2 * p[0] + min(p[1], 4 - p[1])))
 
     def inside(reach):
         return (d + reach >= 0) & (d + reach < DP)
 
-    def peers(reach):
-        return [
-            (d + reach, (m // 4 + hi) % 2 * 4 + (m + y) % 4) for hi, y in others if (reach, hi, y) != (0, 0, 0)
-        ]
+    def for_peers(act):
+        for reach in (3, -3, 2, -2, 1, -1, 0):
+            @pl.when(inside(reach))
+            def _():
+                for hi, y in columns:
+                    if (reach, hi, y) != (0, 0, 0):
+                        act(reach, (d + reach, (m // 4 + hi) % 2 * 4 + (m + y) % 4))
 
     def from_reach(reach):
         return parts.at[pl.ds((reach + REACH) * MP, MP - (reach == 0))]
@@ -123,11 +124,7 @@
 
     parts[...] = jnp.zeros((PEERS, 1, 128), jnp.float32)
     barrier = pltpu.get_barrier_semaphore()
-    for reach in reaches:
-        @pl.when(inside(reach))
-        def _():
-            for pd, pm in peers(reach):
-                pl.semaphore_signal(barrier, inc=1, device_id=(pd, pm), device_id_type=MESH)
+    for_peers(lambda reach, peer: pl.semaphore_signal(barrier, inc=1, device_id=peer, device_id_type=MESH))
     for link in ("up", "down"):
         pl.semaphore_signal(barrier, inc=1, device_id=(target[link], m), device_id_type=MESH)
 
@@ -182,7 +179,8 @@
             second_out[here, :] = new_second
             owned = member(row)
             decay_row = jnp.sum(jnp.where(owned, decay, 0.0), axis=1, keepdims=True)
-            up = new_first / (jnp.sqrt(new_second) * den_scale + den_shift) + decay_row * w
+            root = new_second * lax.rsqrt(new_second)
+            up = new_first / (root * den_scale + den_shift) + decay_row * w
             update[here, :] = up
             w_sum = jnp.sum(w * w, axis=1, keepdims=True)
             u_sum = jnp.sum(up * up, axis=1, keepdims=True)
@@ -194,21 +192,17 @@
     part[...] = total
     parts[REACH * MP + m] = total
 
-    blocks = sum(inside(reach).astype(jnp.int32) for reach in reaches)
+    blocks = sum(inside(reach).astype(jnp.int32) for reach in range(-REACH, REACH + 1))
     pl.semaphore_wait(barrier, blocks * MP + 1)
 
-    for reach in reaches:
-        @pl.when(inside(reach))
-        def _():
-            for pd, pm in peers(reach):
-                pltpu.make_async_remote_copy(
-                    src_ref=part, dst_ref=parts.at[(REACH - reach) * MP + m],
-                    send_sem=part_send.at[REACH - reach], recv_sem=part_recv.at[REACH - reach],
-                    device_id=(pd, pm), device_id_type=MESH,
-                ).start()
+    for_peers(lambda reach, peer: pltpu.make_async_remote_copy(
+        src_ref=part, dst_ref=parts.at[(REACH - reach) * MP + m],
+        send_sem=part_send.at[REACH - reach], recv_sem=part_recv.at[REACH - reach],
+        device_id=peer, device_id_type=MESH,
+    ).start())
 
     def drain(sem):
-        for reach in reaches:
+        for reach in range(-REACH, REACH + 1):
             @pl.when(inside(reach))
             def _():
                 pltpu.make_async_copy(from_reach(reach), from_reach(reach), sem(reach)).wait()

time: 58.2 us -> 57 us (0.979)
  Pallas kernels: 56.8 us -> 55.6 us
    pallas_call x1, Pallas kernels: 51.6 us -> 50.4 us  [local(): pl.pallas_call(kernel, name='lamb_gather', out_shape=[pltpu.VMEM(block, f...]
where the time goes in v3:
time: 57 us; the launch traced here: 56.9 us
  Pallas kernels  55.6 us (98%)
  between operations  1.29 us (2%)
    pallas_call x1, Pallas kernels, local(): pl.pallas_call(kernel, name='lamb_gather', out_shape=[pltpu.VMEM(block, f...  50.4 us
    pallas_call x1, Pallas kernels, local(): pl.pallas_call(store_kernel, name='store', out_shape=[jax.ShapeDtypeStruc...  5.24 us

profile of v3, /device:TPU:1, one launch (start us, length us, event | category | flops | bytes accessed | tf_op | source)
XLA Modules:
  0.0 56.9 jit_solution(3520999205033473590)
XLA Ops:
  1.3 50.4 %lamb_gather.1 = (f32[512,640]{1,0:T(8,128)S(1)}, f32[512,640]{1,0:T(8,128)S(1)}, f32[512,640]{1,0:T(8,128)S(1)}, bf16[8192,640]{1,0:T(8,128)(2,1)S(1)}) custom-call(s32[1]{0:T(128)S(6)} %copy.11.steps_ref, s32[24]{0:T(128)} %rows_hbm.1, s32[24]{0:T(128)} %decay_hbm.1, f32[512,640]{1,0:T(8,128)} %master_hbm.1, f32[512,640]{1,0:T(8,128)} %first_hbm.1, ...), custom_call_target="tpu_custom_call" | custom-call | tf_op jit(solution)/shard_map/lamb_gather/pallas_call | solution.py:306
  51.6 5.2 %store.1 = (f32[512,640]{1,0:T(8,128)}, f32[512,640]{1,0:T(8,128)}, f32[512,640]{1,0:T(8,128)}, bf16[8192,640]{1,0:T(8,128)(2,1)}) custom-call(f32[512,640]{1,0:T(8,128)S(1)} %get-tuple-element.8.refs_0_, f32[512,640]{1,0:T(8,128)S(1)} %get-tuple-element.9.refs_1_, f32[512,640]{1,0:T(8,128)S(1)} %get-tuple-element.10.refs_2_, ...), custom_call_target="tpu_custom_call" | custom-call | tf_op jit(solution)/shard_map/store/pallas_call | solution.py:330
